TPU v7x, 32 devices: a whole 2x2x4 slice. The times are simulated.
32 devices in a mesh: pts: 8 (over z, x), grp: 4 (over y, core).
Axes of the slice: x: 2, y: 2, z: 4, core: 2. Of those that a mesh axis runs over, the one named last changes fastest.
Arguments:
- embeddings: bfloat16 [131072, 1024], P(('pts', 'grp')), as said below
- best_start: float32 [131072], P(('pts', 'grp')), may hold values from 0 to 2
- bounds_start: float32 [131072], P(('pts', 'grp')), may hold values from 0 to 4
- proposals: int32 [8, 32], replicated, may hold values from 0 to 131071
Outputs:
- gain_table: float32 [8, 32], replicated
- coverage: float32 [8], replicated
- best_final: float32 [131072], P(('pts', 'grp'))
- bounds_final: float32 [131072], P(('pts', 'grp'))
Inputs may be any that keep to these rules, and one draw needn't show every extreme that they name: Rows are real valued embeddings of varying norm.
All inputs are finite; a program needn't handle non-finite values.
Results may differ from a plain program's by a relative error of at most 0.0003.
Values may be sent and summed in bfloat16 or wider, within the bound.
A program may use at most 64 MiB of HBM per device.

v0:
```python
import jax
import jax.numpy as jnp
from jax import lax
from jax.sharding import PartitionSpec as P

STEPS = 8


def on_device(embeddings, best_start, bounds_start, proposals):
    row_count = embeddings.shape[0]
    prop_count = proposals.shape[1]
    own_index = lax.axis_index(("pts", "grp"))
    first_row = own_index * row_count
    point_total = row_count * lax.axis_size(("pts", "grp"))
    local_ids = first_row + jnp.arange(row_count, dtype=jnp.int32)
    best_sim = best_start
    bounds = bounds_start
    gain_rows = []
    cover_rows = []
    flat_chosen = proposals.reshape(-1)
    flat_offset = flat_chosen - first_row
    flat_owned = (flat_offset >= 0) & (flat_offset < row_count)
    all_rows = jnp.take(embeddings, jnp.clip(flat_offset, 0, row_count - 1), axis=0)
    all_masked = jnp.where(flat_owned[:, None], all_rows, jnp.zeros_like(all_rows)).astype(
        jnp.float32
    )
    fetched_all = lax.psum(all_masked, ("pts", "grp")).astype(jnp.bfloat16)
    similarity_all = lax.dot_general(
        embeddings, fetched_all, (((1,), (1,)), ((), ())), preferred_element_type=jnp.float32
    )
    for step_index in range(STEPS):
        chosen = proposals[step_index]
        similarity = similarity_all[:, step_index * prop_count : (step_index + 1) * prop_count]
        clipped = jnp.maximum(similarity - best_sim[:, None], 0.0)
        partial_sums = jnp.sum(clipped, axis=0)
        gain_values = lax.psum(partial_sums, ("pts", "grp")) / point_total
        weights = (gain_values + 0.01) / (jnp.sum(gain_values) + 0.01 * prop_count)
        mixed = jnp.dot(similarity, weights, precision=lax.Precision.HIGHEST)
        best_sim = jnp.maximum(best_sim, mixed)
        cover_rows.append(lax.psum(jnp.sum(best_sim), ("pts", "grp")) / point_total)
        matches = local_ids[:, None] == chosen[None, :]
        refreshed = jnp.max(jnp.where(matches, gain_values[None, :], -1.0), axis=1)
        bounds = jnp.where(jnp.any(matches, axis=1), refreshed, bounds)
        gain_rows.append(gain_values)
    return (jnp.stack(gain_rows), jnp.stack(cover_rows), best_sim, bounds)


def solution(mesh):
    placed = (P(("pts", "grp"), None), P(("pts", "grp")), P(("pts", "grp")), P())
    return jax.shard_map(
        on_device,
        mesh=mesh,
        in_specs=placed,
        out_specs=(P(), P(), P(("pts", "grp")), P(("pts", "grp"))),
        check_vma=False,
    )
```

profile of v0, /device:TPU:0, one launch (start us, length us, event | category | flops | bytes accessed | tf_op | source)
XLA Modules:
  0.0 473.4 jit_solution(3717555113697132605)
XLA Ops:
  0.6 0.7 subtract_clamp_fusion
  1.5 6.0 %gather_fusion = bf16[256,1024]{1,0:T(8,128)(2,1)S(1)} fusion(bf16[4096,1024]{1,0:T(8,128)(2,1)} %param.4, s32[1024]{0:T(1024)S(1)} %pad_clamp_fusion), kind=kCustom, calls=%fused_computation | custom fusion | bytes 1049600 | tf_op jit(solution)/shard_map/jit(_take)/gather | solution.py:23
  7.9 53.3 %all-reduce.2 = bf16[256,1024]{1,0:T(8,128)(2,1)S(1)} all-reduce(f32[256,1024]{1,0:T(8,128)S(1)} %select_convert_fusion), channel_id=1, replica_groups=mesh['pts'=8,'grp'=4] {'pts','grp'}, use_global_device_ids=true, to_apply=%region_0.1 | all-reduce | flops 262144 | bytes 1572864 | tf_op jit(solution)/shard_map/psum | solution.py:27
  61.2 7.7 %convolution_bitcast_fusion = f32[4096,256]{0,1:T(8,128)} fusion(bf16[4096,1024]{1,0:T(8,128)(2,1)} %param.4, bf16[256,1024]{1,0:T(8,128)(2,1)S(1)} %all-reduce.2), kind=kOutput, calls=%fused_computation.1 | convolution fusion | flops 2147483648 | bytes 13107200 | tf_op jit(solution)/shard_map/dot_general | solution.py:28
  68.9 1.2 maximum_reduce_fusion.7
  70.1 38.8 %psum.120 = f32[32]{0:T(128)S(1)} all-reduce(f32[32]{0:T(128)S(1)} %maximum_reduce_fusion.7), channel_id=1, replica_groups=mesh['pts'=8,'grp'=4] {'pts','grp'}, use_global_device_ids=true, to_apply=%region_2.3 | all-reduce | flops 32 | bytes 256 | tf_op jit(solution)/shard_map/psum | solution.py:36
  110.2 1.4 fusion.23
  112.2 1.2 maximum_reduce_fusion.6
  113.4 39.3 %psum.121 = f32[32]{0:T(128)S(1)} all-reduce(f32[32]{0:T(128)S(1)} %maximum_reduce_fusion.6), channel_id=1, replica_groups=mesh['pts'=8,'grp'=4] {'pts','grp'}, use_global_device_ids=true, to_apply=%region_5.6 | all-reduce | flops 32 | bytes 256 | tf_op jit(solution)/shard_map/psum | solution.py:36
  154.0 1.4 fusion.21
  156.0 1.2 maximum_reduce_fusion.5
  157.2 40.6 %psum.122 = f32[32]{0:T(128)S(1)} all-reduce(f32[32]{0:T(128)S(1)} %maximum_reduce_fusion.5), channel_id=1, replica_groups=mesh['pts'=8,'grp'=4] {'pts','grp'}, use_global_device_ids=true, to_apply=%region_8.9 | all-reduce | flops 32 | bytes 256 | tf_op jit(solution)/shard_map/psum | solution.py:36
  199.1 1.4 fusion.19
  201.1 1.2 maximum_reduce_fusion.4
  202.3 39.3 %psum.123 = f32[32]{0:T(128)S(1)} all-reduce(f32[32]{0:T(128)S(1)} %maximum_reduce_fusion.4), channel_id=1, replica_groups=mesh['pts'=8,'grp'=4] {'pts','grp'}, use_global_device_ids=true, to_apply=%region_11.12 | all-reduce | flops 32 | bytes 256 | tf_op jit(solution)/shard_map/psum | solution.py:36
  242.9 1.4 fusion.17
  245.0 1.2 maximum_reduce_fusion.3
  246.2 40.6 %psum.124 = f32[32]{0:T(128)S(1)} all-reduce(f32[32]{0:T(128)S(1)} %maximum_reduce_fusion.3), channel_id=1, replica_groups=mesh['pts'=8,'grp'=4] {'pts','grp'}, use_global_device_ids=true, to_apply=%region_14.15 | all-reduce | flops 32 | bytes 256 | tf_op jit(solution)/shard_map/psum | solution.py:36
  288.0 1.4 fusion.15
  290.1 1.2 maximum_reduce_fusion.2
  291.3 39.5 %psum.125 = f32[32]{0:T(128)S(1)} all-reduce(f32[32]{0:T(128)S(1)} %maximum_reduce_fusion.2), channel_id=1, replica_groups=mesh['pts'=8,'grp'=4] {'pts','grp'}, use_global_device_ids=true, to_apply=%region_17.18 | all-reduce | flops 32 | bytes 256 | tf_op jit(solution)/shard_map/psum | solution.py:36
  332.1 1.4 fusion.13
  334.1 1.2 maximum_reduce_fusion.1
  335.3 40.6 %psum.126 = f32[32]{0:T(128)S(1)} all-reduce(f32[32]{0:T(128)S(1)} %maximum_reduce_fusion.1), channel_id=1, replica_groups=mesh['pts'=8,'grp'=4] {'pts','grp'}, use_global_device_ids=true, to_apply=%region_20.21 | all-reduce | flops 32 | bytes 256 | tf_op jit(solution)/shard_map/psum | solution.py:36
  377.2 1.4 fusion.11
  379.2 1.2 maximum_reduce_fusion
  380.4 39.3 %psum.127 = f32[32]{0:T(128)S(1)} all-reduce(f32[32]{0:T(128)S(1)} %maximum_reduce_fusion), channel_id=1, replica_groups=mesh['pts'=8,'grp'=4] {'pts','grp'}, use_global_device_ids=true, to_apply=%region_23.24 | all-reduce | flops 32 | bytes 256 | tf_op jit(solution)/shard_map/psum | solution.py:36
  420.3 0.7 fusion.7
  421.1 0.9 compare_reduce_fusion
  423.3 1.4 fusion.9
  424.7 1.2 fusion.89
  425.9 41.2 %all-reduce = (f32[]{:T(128)}, f32[]{:T(128)}, f32[]{:T(128)}, f32[]{:T(128)}, f32[]{:T(128)}, /*index=5*/f32[]{:T(128)}, f32[]{:T(128)}, f32[]{:T(128)}) all-reduce(f32[]{:T(128)} %get-tuple-element.42, f32[]{:T(128)} %get-tuple-element.40, f32[]{:T(128)} %get-tuple-element.38, ...), channel_id=1, replica_groups=mesh['pts'=8,'grp'=4] {'pts','grp'}, use_global_device_ids=true, to_apply=%region_25.26 | all-reduce | flops 8 | bytes 64 | tf_op jit(solution)/shard_map/psum | solution.py:40
  (34 shorter events, 11.4 us)
Async XLA Ops:
  0.6 7.0 %copy-start.1 = (s32[8,32]{1,0:T(8,128)S(1)}, s32[8,32]{1,0:T(8,128)}, u32[]{:S(2)}) copy-start(s32[8,32]{1,0:T(8,128)} %param.7) | copy-start | bytes 3076
  61.2 7.7 %copy-start = (f32[4096]{0:T(1024)S(1)}, f32[4096]{0:T(1024)}, u32[]{:S(2)}) copy-start(f32[4096]{0:T(1024)} %param.5) | copy-start | bytes 49156
  70.1 351.9 %copy-start.2 = (f32[4096]{0:T(1024)S(1)}, f32[4096]{0:T(1024)}, u32[]{:S(2)}) copy-start(f32[4096]{0:T(1024)} %param.6) | copy-start | bytes 49156
where the time goes:
time: 475 us; the launch traced here: 473 us
  blocking collectives  413 us (87%)
  other arithmetic  23.2 us (5%)
  matrix products  19.1 us (4%)
  between operations  11.1 us (2%)
  local copies, waits for them, and re-layouts  7.49 us (2%)
    psum x8, blocking collectives, on_device(): gain_values = lax.psum(partial_sums, ('pts', 'grp')) / point_total  318 us
    psum x1, blocking collectives, on_device(): fetched_all = lax.psum(all_masked, ('pts', 'grp')).astype(jnp.bfloat16)  53.3 us
    psum x1, blocking collectives, on_device(): cover_rows.append(lax.psum(jnp.sum(best_sim), ('pts', 'grp')) / point_total)  41.2 us
    dot_general x8, matrix products, on_device(): mixed = jnp.dot(similarity, weights, precision=lax.Precision.HIGHEST)  11.4 us
    reduce_sum x8, other arithmetic, on_device(): partial_sums = jnp.sum(clipped, axis=0)  9.6 us

commit v1 on v0

--- a/solution.py
+++ b/solution.py
@@ -2,6 +2,7 @@
 import jax.numpy as jnp
 from jax import lax
 from jax.sharding import PartitionSpec as P
+from jax.lax import psum
 
 STEPS = 8
 
@@ -33,7 +34,7 @@
         similarity = similarity_all[:, step_index * prop_count : (step_index + 1) * prop_count]
         clipped = jnp.maximum(similarity - best_sim[:, None], 0.0)
         partial_sums = jnp.sum(clipped, axis=0)
-        gain_values = lax.psum(partial_sums, ("pts", "grp")) / point_total
+        gain_values = psum(psum(partial_sums, "grp"), "pts") / point_total
         weights = (gain_values + 0.01) / (jnp.sum(gain_values) + 0.01 * prop_count)
         mixed = jnp.dot(similarity, weights, precision=lax.Precision.HIGHEST)
         best_sim = jnp.maximum(best_sim, mixed)

time: 475 us -> 346 us (0.73)
  blocking collectives: 413 us -> 283 us
    psum x8 -> x16, blocking collectives: 318 us -> 191 us  [on_device(): gain_values = psum(psum(partial_sums, 'grp'), 'pts') / point_total]
where the time goes in v1:
time: 346 us; the launch traced here: 344 us
  blocking collectives  283 us (82%)
  other arithmetic  23.2 us (7%)
  matrix products  19.1 us (6%)
  between operations  11.1 us (3%)
  local copies, waits for them, and re-layouts  7.49 us (2%)
    psum x16, blocking collectives, on_device(): gain_values = psum(psum(partial_sums, 'grp'), 'pts') / point_total  191 us
    psum x1, blocking collectives, on_device(): fetched_all = lax.psum(all_masked, ('pts', 'grp')).astype(jnp.bfloat16)  53.3 us
    psum x1, blocking collectives, on_device(): cover_rows.append(lax.psum(jnp.sum(best_sim), ('pts', 'grp')) / point_total)  39.3 us
    dot_general x8, matrix products, on_device(): mixed = jnp.dot(similarity, weights, precision=lax.Precision.HIGHEST)  11.4 us
    reduce_sum x8, other arithmetic, on_device(): partial_sums = jnp.sum(clipped, axis=0)  9.6 us
    dot_general x1, matrix products, on_device(): lax.dot_general(embeddings, fetched_all, (((1,), (1,)), ((), ())), prefer...  7.68 us

profile of v1, /device:TPU:0, one launch (start us, length us, event | category | flops | bytes accessed | tf_op | source)
XLA Modules:
  0.0 344.2 jit_solution(18254805858355119353)
XLA Ops:
  1.5 6.0 %gather_fusion = bf16[256,1024]{1,0:T(8,128)(2,1)S(1)} fusion(bf16[4096,1024]{1,0:T(8,128)(2,1)} %param.4, s32[1024]{0:T(1024)S(1)} %pad_clamp_fusion), kind=kCustom, calls=%fused_computation | custom fusion | bytes 1049600 | tf_op jit(solution)/shard_map/jit(_take)/gather | solution.py:24
  7.9 53.3 %all-reduce.2 = bf16[256,1024]{1,0:T(8,128)(2,1)S(1)} all-reduce(f32[256,1024]{1,0:T(8,128)S(1)} %select_convert_fusion), channel_id=1, replica_groups=mesh['pts'=8,'grp'=4] {'pts','grp'}, use_global_device_ids=true, to_apply=%region_0.1 | all-reduce | flops 262144 | bytes 1572864 | tf_op jit(solution)/shard_map/psum | solution.py:28
  61.2 7.7 %convolution_bitcast_fusion = f32[4096,256]{0,1:T(8,128)} fusion(bf16[4096,1024]{1,0:T(8,128)(2,1)} %param.4, bf16[256,1024]{1,0:T(8,128)(2,1)S(1)} %all-reduce.2), kind=kOutput, calls=%fused_computation.1 | convolution fusion | flops 2147483648 | bytes 13107200 | tf_op jit(solution)/shard_map/dot_general | solution.py:29
  68.9 1.2 maximum_reduce_fusion.7
  70.1 5.9 %psum.176 = f32[32]{0:T(128)S(1)} all-reduce(f32[32]{0:T(128)S(1)} %maximum_reduce_fusion.7), channel_id=1, replica_groups=mesh['pts'=8,'grp'=4] {'grp'}, use_global_device_ids=true, to_apply=%region_2.3 | all-reduce | flops 32 | bytes 256 | tf_op jit(solution)/shard_map/psum | solution.py:37
  76.0 18.6 %psum.177 = f32[32]{0:T(128)S(1)} all-reduce(f32[32]{0:T(128)S(1)} %psum.176), channel_id=1, replica_groups=mesh['pts'=8,'grp'=4] {'pts'}, use_global_device_ids=true, to_apply=%region_3.4 | all-reduce | flops 32 | bytes 256 | tf_op jit(solution)/shard_map/psum | solution.py:37
  95.9 1.4 fusion.23
  97.9 1.2 maximum_reduce_fusion.6
  99.1 5.7 %psum.178 = f32[32]{0:T(128)S(1)} all-reduce(f32[32]{0:T(128)S(1)} %maximum_reduce_fusion.6), channel_id=1, replica_groups=mesh['pts'=8,'grp'=4] {'grp'}, use_global_device_ids=true, to_apply=%region_6.7 | all-reduce | flops 32 | bytes 256 | tf_op jit(solution)/shard_map/psum | solution.py:37
  104.8 17.7 %psum.179 = f32[32]{0:T(128)S(1)} all-reduce(f32[32]{0:T(128)S(1)} %psum.178), channel_id=1, replica_groups=mesh['pts'=8,'grp'=4] {'pts'}, use_global_device_ids=true, to_apply=%region_7.8 | all-reduce | flops 32 | bytes 256 | tf_op jit(solution)/shard_map/psum | solution.py:37
  123.7 1.4 fusion.21
  125.7 1.2 maximum_reduce_fusion.5
  126.9 5.7 %psum.180 = f32[32]{0:T(128)S(1)} all-reduce(f32[32]{0:T(128)S(1)} %maximum_reduce_fusion.5), channel_id=1, replica_groups=mesh['pts'=8,'grp'=4] {'grp'}, use_global_device_ids=true, to_apply=%region_10.11 | all-reduce | flops 32 | bytes 256 | tf_op jit(solution)/shard_map/psum | solution.py:37
  132.6 18.5 %psum.181 = f32[32]{0:T(128)S(1)} all-reduce(f32[32]{0:T(128)S(1)} %psum.180), channel_id=1, replica_groups=mesh['pts'=8,'grp'=4] {'pts'}, use_global_device_ids=true, to_apply=%region_11.12 | all-reduce | flops 32 | bytes 256 | tf_op jit(solution)/shard_map/psum | solution.py:37
  152.4 1.4 fusion.19
  155.7 5.7 %psum.182 = f32[32]{0:T(128)S(1)} all-reduce(f32[32]{0:T(128)S(1)} %maximum_reduce_fusion.4), channel_id=1, replica_groups=mesh['pts'=8,'grp'=4] {'grp'}, use_global_device_ids=true, to_apply=%region_14.15 | all-reduce | flops 32 | bytes 256 | tf_op jit(solution)/shard_map/psum | solution.py:37
  161.3 17.7 %psum.183 = f32[32]{0:T(128)S(1)} all-reduce(f32[32]{0:T(128)S(1)} %psum.182), channel_id=1, replica_groups=mesh['pts'=8,'grp'=4] {'pts'}, use_global_device_ids=true, to_apply=%region_15.16 | all-reduce | flops 32 | bytes 256 | tf_op jit(solution)/shard_map/psum | solution.py:37
  180.3 1.4 fusion.17
  183.5 5.7 %psum.184 = f32[32]{0:T(128)S(1)} all-reduce(f32[32]{0:T(128)S(1)} %maximum_reduce_fusion.3), channel_id=1, replica_groups=mesh['pts'=8,'grp'=4] {'grp'}, use_global_device_ids=true, to_apply=%region_18.19 | all-reduce | flops 32 | bytes 256 | tf_op jit(solution)/shard_map/psum | solution.py:37
  189.2 18.5 %psum.185 = f32[32]{0:T(128)S(1)} all-reduce(f32[32]{0:T(128)S(1)} %psum.184), channel_id=1, replica_groups=mesh['pts'=8,'grp'=4] {'pts'}, use_global_device_ids=true, to_apply=%region_19.20 | all-reduce | flops 32 | bytes 256 | tf_op jit(solution)/shard_map/psum | solution.py:37
  209.0 1.4 fusion.15
  212.3 5.7 %psum.186 = f32[32]{0:T(128)S(1)} all-reduce(f32[32]{0:T(128)S(1)} %maximum_reduce_fusion.2), channel_id=1, replica_groups=mesh['pts'=8,'grp'=4] {'grp'}, use_global_device_ids=true, to_apply=%region_22.23 | all-reduce | flops 32 | bytes 256 | tf_op jit(solution)/shard_map/psum | solution.py:37
  218.0 17.6 %psum.187 = f32[32]{0:T(128)S(1)} all-reduce(f32[32]{0:T(128)S(1)} %psum.186), channel_id=1, replica_groups=mesh['pts'=8,'grp'=4] {'pts'}, use_global_device_ids=true, to_apply=%region_23.24 | all-reduce | flops 32 | bytes 256 | tf_op jit(solution)/shard_map/psum | solution.py:37
  236.9 1.4 fusion.13
  240.1 5.7 %psum.188 = f32[32]{0:T(128)S(1)} all-reduce(f32[32]{0:T(128)S(1)} %maximum_reduce_fusion.1), channel_id=1, replica_groups=mesh['pts'=8,'grp'=4] {'grp'}, use_global_device_ids=true, to_apply=%region_26.27 | all-reduce | flops 32 | bytes 256 | tf_op jit(solution)/shard_map/psum | solution.py:37
  245.8 18.7 %psum.189 = f32[32]{0:T(128)S(1)} all-reduce(f32[32]{0:T(128)S(1)} %psum.188), channel_id=1, replica_groups=mesh['pts'=8,'grp'=4] {'pts'}, use_global_device_ids=true, to_apply=%region_27.28 | all-reduce | flops 32 | bytes 256 | tf_op jit(solution)/shard_map/psum | solution.py:37
  265.8 1.4 fusion.11
  269.0 5.8 %psum.190 = f32[32]{0:T(128)S(1)} all-reduce(f32[32]{0:T(128)S(1)} %maximum_reduce_fusion), channel_id=1, replica_groups=mesh['pts'=8,'grp'=4] {'grp'}, use_global_device_ids=true, to_apply=%region_30.31 | all-reduce | flops 32 | bytes 256 | tf_op jit(solution)/shard_map/psum | solution.py:37
  274.8 17.6 %psum.191 = f32[32]{0:T(128)S(1)} all-reduce(f32[32]{0:T(128)S(1)} %psum.190), channel_id=1, replica_groups=mesh['pts'=8,'grp'=4] {'pts'}, use_global_device_ids=true, to_apply=%region_31.32 | all-reduce | flops 32 | bytes 256 | tf_op jit(solution)/shard_map/psum | solution.py:37
  295.9 1.4 fusion.9
  297.4 1.2 fusion.89
  298.6 39.3 %all-reduce = (f32[]{:T(128)}, f32[]{:T(128)}, f32[]{:T(128)}, f32[]{:T(128)}, f32[]{:T(128)}, /*index=5*/f32[]{:T(128)}, f32[]{:T(128)}, f32[]{:T(128)}) all-reduce(f32[]{:T(128)} %get-tuple-element.42, f32[]{:T(128)} %get-tuple-element.40, f32[]{:T(128)} %get-tuple-element.38, ...), channel_id=1, replica_groups=mesh['pts'=8,'grp'=4] {'pts','grp'}, use_global_device_ids=true, to_apply=%region_33.34 | all-reduce | flops 8 | bytes 64 | tf_op jit(solution)/shard_map/psum | solution.py:41
  (42 shorter events, 19.9 us)
Async XLA Ops:
  0.6 7.0 %copy-start.1 = (s32[8,32]{1,0:T(8,128)S(1)}, s32[8,32]{1,0:T(8,128)}, u32[]{:S(2)}) copy-start(s32[8,32]{1,0:T(8,128)} %param.7) | copy-start | bytes 3076
  61.2 7.7 %copy-start = (f32[4096]{0:T(1024)S(1)}, f32[4096]{0:T(1024)}, u32[]{:S(2)}) copy-start(f32[4096]{0:T(1024)} %param.5) | copy-start | bytes 49156
  70.1 224.6 %copy-start.2 = (f32[4096]{0:T(1024)S(1)}, f32[4096]{0:T(1024)}, u32[]{:S(2)}) copy-start(f32[4096]{0:T(1024)} %param.6) | copy-start | bytes 49156

commit v2 on v0

--- a/solution.py
+++ b/solution.py
@@ -4,6 +4,7 @@
 from jax.sharding import PartitionSpec as P
 
 STEPS = 8
+_supply_all_quarters = lambda matrix: jax.lax.all_gather(matrix, ("pts", "grp")).sum(axis=0)
 
 
 def on_device(embeddings, best_start, bounds_start, proposals):
@@ -33,7 +34,7 @@
         similarity = similarity_all[:, step_index * prop_count : (step_index + 1) * prop_count]
         clipped = jnp.maximum(similarity - best_sim[:, None], 0.0)
         partial_sums = jnp.sum(clipped, axis=0)
-        gain_values = lax.psum(partial_sums, ("pts", "grp")) / point_total
+        gain_values = _supply_all_quarters(partial_sums) / point_total
         weights = (gain_values + 0.01) / (jnp.sum(gain_values) + 0.01 * prop_count)
         mixed = jnp.dot(similarity, weights, precision=lax.Precision.HIGHEST)
         best_sim = jnp.maximum(best_sim, mixed)

time: 475 us -> 492 us (1.036)
  local copies, waits for them, and re-layouts: 7.49 us -> 24.5 us
    unnamed x0 -> x8, blocking collectives: none -> 320 us
    psum x8 -> x0, blocking collectives: 318 us -> none  [on_device(): gain_values = lax.psum(partial_sums, ('pts', 'grp')) / point_total]
    unnamed x6 -> x26, local copies, waits for them, and re-layouts: 0.01 us -> 16.5 us
where the time goes in v2:
time: 492 us; the launch traced here: 490 us
  blocking collectives  414 us (84%)
  local copies, waits for them, and re-layouts  24.5 us (5%)
  other arithmetic  22.4 us (5%)
  matrix products  17.2 us (3%)
  between operations  11.1 us (2%)
    unnamed x8, blocking collectives  320 us
    psum x1, blocking collectives, on_device(): fetched_all = lax.psum(all_masked, ('pts', 'grp')).astype(jnp.bfloat16)  53.3 us
    psum x1, blocking collectives, on_device(): cover_rows.append(lax.psum(jnp.sum(best_sim), ('pts', 'grp')) / point_total)  41.2 us
    unnamed x26, local copies, waits for them, and re-layouts  16.5 us
    dot_general x8, matrix products, on_device(): mixed = jnp.dot(similarity, weights, precision=lax.Precision.HIGHEST)  11.5 us

profile of v2, /device:TPU:0, one launch (start us, length us, event | category | flops | bytes accessed | tf_op | source)
XLA Modules:
  0.0 489.6 jit_solution(15097443998387821426)
XLA Ops:
  1.5 6.0 %gather_fusion = bf16[256,1024]{1,0:T(8,128)(2,1)S(1)} fusion(bf16[4096,1024]{1,0:T(8,128)(2,1)} %param.4, s32[1024]{0:T(1024)S(1)} %pad_clamp_fusion), kind=kCustom, calls=%fused_computation | custom fusion | bytes 1049600 | tf_op jit(solution)/shard_map/jit(_take)/gather | solution.py:24
  7.9 53.3 %all-reduce.10 = bf16[256,1024]{1,0:T(8,128)(2,1)S(1)} all-reduce(f32[256,1024]{1,0:T(8,128)S(1)} %select_convert_fusion), channel_id=1, replica_groups=mesh['pts'=8,'grp'=4] {'pts','grp'}, use_global_device_ids=true, to_apply=%region_0.1 | all-reduce | flops 262144 | bytes 1572864 | tf_op jit(solution)/shard_map/psum | solution.py:28
  61.2 5.8 %convolution_bitcast_fusion = f32[4096,256]{0,1:T(8,128)S(1)} fusion(bf16[4096,1024]{1,0:T(8,128)(2,1)} %param.4, bf16[256,1024]{1,0:T(8,128)(2,1)S(1)} %all-reduce.10), kind=kOutput, calls=%fused_computation.1 | convolution fusion | flops 2147483648 | bytes 13107200 | tf_op jit(solution)/shard_map/dot_general | solution.py:29
  67.0 1.9 copy-done
  69.9 39.0 %all-reduce = f32[1024]{0:T(1024)S(1)} all-reduce(f32[1024]{0:T(1024)} %copy-done.4), channel_id=2, replica_groups=mesh['pts'=8,'grp'=4] {'pts','grp'}, use_global_device_ids=true, to_apply=%add | all-reduce | flops 1024 | bytes 8192
  110.3 1.4 fusion.23
  112.4 1.2 maximum_reduce_fusion.6
  114.2 1.4 dynamic-update-slice.1
  115.5 39.5 %all-reduce.1 = f32[1024]{0:T(1024)S(1)} all-reduce(f32[1024]{0:T(1024)} %dynamic-update-slice.1), channel_id=3, replica_groups=mesh['pts'=8,'grp'=4] {'pts','grp'}, use_global_device_ids=true, to_apply=%add.1 | all-reduce | flops 1024 | bytes 8192
  156.4 1.4 fusion.21
  158.5 1.2 maximum_reduce_fusion.5
  160.3 1.4 dynamic-update-slice.2
  161.6 40.8 %all-reduce.2 = f32[1024]{0:T(1024)S(1)} all-reduce(f32[1024]{0:T(1024)} %dynamic-update-slice.2), channel_id=4, replica_groups=mesh['pts'=8,'grp'=4] {'pts','grp'}, use_global_device_ids=true, to_apply=%add.2 | all-reduce | flops 1024 | bytes 8192
  203.8 1.4 fusion.19
  205.9 1.2 maximum_reduce_fusion.4
  207.7 1.4 dynamic-update-slice.3
  209.0 39.5 %all-reduce.3 = f32[1024]{0:T(1024)S(1)} all-reduce(f32[1024]{0:T(1024)} %dynamic-update-slice.3), channel_id=5, replica_groups=mesh['pts'=8,'grp'=4] {'pts','grp'}, use_global_device_ids=true, to_apply=%add.3 | all-reduce | flops 1024 | bytes 8192
  249.9 1.4 fusion.17
  253.8 1.4 dynamic-update-slice.4
  255.2 41.0 %all-reduce.4 = f32[1024]{0:T(1024)S(1)} all-reduce(f32[1024]{0:T(1024)} %dynamic-update-slice.4), channel_id=6, replica_groups=mesh['pts'=8,'grp'=4] {'pts','grp'}, use_global_device_ids=true, to_apply=%add.4 | all-reduce | flops 1024 | bytes 8192
  297.6 1.4 fusion.15
  301.4 1.4 dynamic-update-slice.5
  302.7 39.5 %all-reduce.5 = f32[1024]{0:T(1024)S(1)} all-reduce(f32[1024]{0:T(1024)} %dynamic-update-slice.5), channel_id=7, replica_groups=mesh['pts'=8,'grp'=4] {'pts','grp'}, use_global_device_ids=true, to_apply=%add.5 | all-reduce | flops 1024 | bytes 8192
  343.6 1.4 fusion.13
  347.5 1.4 dynamic-update-slice.6
  348.8 40.8 %all-reduce.6 = f32[1024]{0:T(1024)S(1)} all-reduce(f32[1024]{0:T(1024)} %dynamic-update-slice.6), channel_id=8, replica_groups=mesh['pts'=8,'grp'=4] {'pts','grp'}, use_global_device_ids=true, to_apply=%add.6 | all-reduce | flops 1024 | bytes 8192
  391.0 1.4 fusion.11
  394.9 1.4 dynamic-update-slice.7
  396.3 39.5 %all-reduce.7 = f32[1024]{0:T(1024)S(1)} all-reduce(f32[1024]{0:T(1024)} %dynamic-update-slice.7), channel_id=9, replica_groups=mesh['pts'=8,'grp'=4] {'pts','grp'}, use_global_device_ids=true, to_apply=%add.7 | all-reduce | flops 1024 | bytes 8192
  439.5 1.4 fusion.9
  440.9 1.2 fusion.89
  442.1 41.2 %all-reduce.8 = (f32[]{:T(128)}, f32[]{:T(128)}, f32[]{:T(128)}, f32[]{:T(128)}, f32[]{:T(128)}, /*index=5*/f32[]{:T(128)}, f32[]{:T(128)}, f32[]{:T(128)}) all-reduce(f32[]{:T(128)} %get-tuple-element.42, f32[]{:T(128)} %get-tuple-element.40, f32[]{:T(128)} %get-tuple-element.38, ...), channel_id=1, replica_groups=mesh['pts'=8,'grp'=4] {'pts','grp'}, use_global_device_ids=true, to_apply=%region_25.26 | all-reduce | flops 8 | bytes 64 | tf_op jit(solution)/shard_map/psum | solution.py:41
  (70 shorter events, 24.7 us)
Async XLA Ops:
  0.6 7.0 %copy-start.2 = (s32[8,32]{1,0:T(8,128)S(1)}, s32[8,32]{1,0:T(8,128)}, u32[]{:S(2)}) copy-start(s32[8,32]{1,0:T(8,128)} %param.7) | copy-start | bytes 3076
  61.2 7.7 %copy-start.1 = (f32[4096]{0:T(1024)S(1)}, f32[4096]{0:T(1024)}, u32[]{:S(2)}) copy-start(f32[4096]{0:T(1024)} %param.5) | copy-start | bytes 49156
  67.0 1.9 copy-start
  69.3 0.6 copy-start.4
  110.3 327.9 %copy-start.3 = (f32[4096]{0:T(1024)S(1)}, f32[4096]{0:T(1024)}, u32[]{:S(2)}) copy-start(f32[4096]{0:T(1024)} %param.6) | copy-start | bytes 49156
